TPU v7x, 8 devices: a whole 2x2x1 slice. The times are simulated.
8 devices in a mesh: tp: 2 (over z, y), dp: 4 (over x, core).
Axes of the slice: x: 2, y: 2, z: 1, core: 2. Of those that a mesh axis runs over, the one named last changes fastest.
Arguments:
- x: bfloat16 [8192, 5120], P(('dp', 'tp'))
- w_gate: bfloat16 [5120, 14336], P('dp', 'tp')
- w_up: bfloat16 [5120, 14336], P('dp', 'tp')
- w_down: bfloat16 [14336, 5120], P('tp', 'dp')
Outputs:
- output: bfloat16 [8192, 5120], P(('dp', 'tp'))
All inputs are finite; a program needn't handle non-finite values.
Results may differ from a plain program's by a relative error of at most 0.0130042.
Values are sent between devices in bfloat16 or wider.
A program may use at most 1 GiB of HBM per device.

v0:
```python
import jax
import jax.numpy as jnp
from jax import lax
from jax.sharding import PartitionSpec as P


def solution(mesh):
    nt = mesh.shape["tp"]
    nd = mesh.shape["dp"]

    def body(x, wg, wu, wd):
        r, d = x.shape
        dc = d // nd
        xt = lax.all_gather(x, "tp", axis=0, tiled=True)
        xc = lax.all_to_all(xt, "dp", 1, 0, tiled=True)
        pa = jnp.dot(xc, wg, preferred_element_type=jnp.float32).astype(jnp.bfloat16)
        pb = jnp.dot(xc, wu, preferred_element_type=jnp.float32).astype(jnp.bfloat16)
        a = lax.psum_scatter(pa, "dp", scatter_dimension=0, tiled=True).astype(jnp.float32)
        b = lax.psum_scatter(pb, "dp", scatter_dimension=0, tiled=True).astype(jnp.float32)
        h = (jax.nn.silu(a) * b).astype(jnp.bfloat16)
        hg = lax.all_gather(h, "dp", axis=0, tiled=True)
        po = jnp.dot(hg, wd, preferred_element_type=jnp.float32).astype(jnp.bfloat16)
        po = po.reshape(nd, nt, r, dc)
        ps = lax.psum_scatter(po, "tp", scatter_dimension=1, tiled=True)
        o = lax.all_to_all(ps.reshape(nd, r, dc), "dp", 0, 0, tiled=True)
        o = o.transpose(1, 0, 2).reshape(r, d)
        return (x.astype(jnp.float32) + o.astype(jnp.float32)).astype(jnp.bfloat16)

    return jax.shard_map(body, mesh=mesh, in_specs=(P(("dp", "tp"), None), P("dp", "tp"), P("dp", "tp"), P("tp", "dp")), out_specs=P(("dp", "tp"), None), check_vma=False)
```

profile of v0, /device:TPU:0, one launch (start us, length us, event | category | flops | bytes accessed | tf_op | source)
XLA Modules:
  0.0 3686.1 jit_solution(14922231326308797736)
XLA Ops:
  6.5 0.0 all-gather.3.cloned.1.call-start
  6.5 14.4 copy.12
  20.9 0.0 all-gather.3.cloned.1.call-update
  21.0 0.0 reduce-scatter.6.cloned.1.call-start
  21.0 247.9 %all-gather.3.cloned.1.call-done = bf16[2048,5120]{0,1:T(8,128)(2,1)} async-done(((bf16[1024,5120]{0,1:T(8,128)(2,1)}), bf16[2048,5120]{0,1:T(8,128)(2,1)}) %all-gather.3.cloned.1.call-update) | async-done | bytes 20971536 | tf_op jit(solution)/shard_map/all_gather | solution.py:14
  268.9 240.5 %all_to_all.24 = bf16[2048,4,1280]{0,2,1:T(8,128)(2,1)} all-to-all(bf16[2048,4,1280]{0,2,1:T(8,128)(2,1)} %bitcast.31), channel_id=1, replica_groups=mesh['tp'=2,'dp'=4] {'dp'}, dimensions={1} | all-to-all | bytes 41943040 | tf_op jit(solution)/shard_map/all_to_all | solution.py:15
  509.4 27.9 copy.14
  537.3 164.1 %convolution_convert_fusion.1 = bf16[8192,7168]{1,0:T(8,128)(2,1)} fusion(bf16[8192,1280]{1,0:T(8,128)(2,1)} %bitcast.29, bf16[1280,7168]{1,0:T(8,128)(2,1)} %param.5), kind=kOutput, calls=%fused_computation.1 | convolution fusion | flops 150382575616 | bytes 156762112 | tf_op jit(solution)/shard_map/dot_general | solution.py:16
  701.4 0.0 reduce-scatter.6.cloned.1.call-update
  701.4 0.2 reduce-scatter.8.cloned.1.call-start
  701.6 164.2 %convolution_convert_fusion = bf16[8192,7168]{1,0:T(8,128)(2,1)} fusion(bf16[8192,1280]{1,0:T(8,128)(2,1)} %bitcast.30, bf16[1280,7168]{1,0:T(8,128)(2,1)} %param.6), kind=kOutput, calls=%fused_computation | convolution fusion | flops 150382575616 | bytes 156762112 | tf_op jit(solution)/shard_map/dot_general | solution.py:17
  865.8 0.0 reduce-scatter.8.cloned.1.call-update
  865.9 0.0 all-gather.5.cloned.1.call-start
  865.9 574.3 %reduce-scatter.6.cloned.1.call-done = bf16[2048,7168]{1,0:T(8,128)(2,1)} async-done(((bf16[8192,7168]{1,0:T(8,128)(2,1)}), bf16[2048,7168]{1,0:T(8,128)(2,1)}) %reduce-scatter.6.cloned.1.call-update) | async-done | bytes 29360144 | tf_op jit(solution)/shard_map/reduce_scatter | solution.py:18
  1440.2 742.3 %reduce-scatter.8.cloned.1.call-done = bf16[2048,7168]{1,0:T(8,128)(2,1)} async-done(((bf16[8192,7168]{1,0:T(8,128)(2,1)}), bf16[2048,7168]{1,0:T(8,128)(2,1)}) %reduce-scatter.8.cloned.1.call-update) | async-done | bytes 29360144 | tf_op jit(solution)/shard_map/reduce_scatter | solution.py:19
  2182.5 29.9 fusion.4
  2212.4 0.0 all-gather.5.cloned.1.call-update
  2212.5 0.3 all-reduce.3.cloned.1.call-start
  2212.7 675.0 %all-gather.5.cloned.1.call-done = bf16[8192,7168]{1,0:T(8,128)(2,1)} async-done(((bf16[2048,7168]{1,0:T(8,128)(2,1)}), bf16[8192,7168]{1,0:T(8,128)(2,1)}) %all-gather.5.cloned.1.call-update) | async-done | bytes 117440528 | tf_op jit(solution)/shard_map/all_gather | solution.py:21
  2887.8 164.3 %convolution_convert_fusion.2 = bf16[8192,1280]{1,0:T(8,128)(2,1)} fusion(bf16[8192,7168]{1,0:T(8,128)(2,1)} %all-gather.5.cloned.1.call-done, bf16[7168,1280]{1,0:T(8,128)(2,1)} %param.7), kind=kOutput, calls=%fused_computation.9 | convolution fusion | flops 150334341120 | bytes 156762112 | tf_op jit(solution)/shard_map/dot_general | solution.py:22
  3052.1 0.0 copy-start
  3052.1 0.0 all-reduce.3.cloned.1.call-update
  3052.1 0.6 copy-done
  3052.7 0.7 dynamic-slice
  3053.4 461.0 %all-reduce.3.cloned.1.call-done = bf16[4,2,1024,1280]{3,2,1,0:T(8,128)(2,1)} async-done(((bf16[4,2,1024,1280]{3,2,1,0:T(8,128)(2,1)}), bf16[4,2,1024,1280]{3,2,1,0:T(8,128)(2,1)}) %all-reduce.3.cloned.1.call-update) | async-done | bytes 20971536
  3514.4 9.3 constant_dynamic-slice_fusion
  3523.7 14.4 copy.15
  3538.0 0.0 slice-start
  3538.0 0.0 slice-start.1
  3538.0 0.0 slice-start.2
  3538.1 120.8 %all_to_all.25 = bf16[4,1024,1280]{1,2,0:T(8,128)(2,1)S(1)} all-to-all(bf16[4,1024,1280]{1,2,0:T(8,128)(2,1)} %bitcast.27), channel_id=1, replica_groups=mesh['tp'=2,'dp'=4] {'dp'}, dimensions={0} | all-to-all | bytes 20971520 | tf_op jit(solution)/shard_map/all_to_all | solution.py:25
  3658.8 0.0 slice-done
  3658.8 0.0 slice-done.1
  3658.8 0.0 slice-done.2
  3658.8 7.1 fusion.5
  3665.9 13.7 copy.16
  (1 shorter events, 0.0 us)
Async XLA Ops:
  6.5 262.4 %all-gather.3.cloned.1.call-start = ((), (), s32[]{:S(2)}) async-start(), calls=%async_computation.4 | async-start | bytes 31457280 | tf_op jit(solution)/shard_map/all_gather | solution.py:14
  21.0 1419.2 %reduce-scatter.6.cloned.1.call-start = ((), (), s32[]{:S(2)}) async-start(), calls=%async_computation.5 | async-start | bytes 146800640 | tf_op jit(solution)/shard_map/reduce_scatter | solution.py:18
  701.4 1481.1 %reduce-scatter.8.cloned.1.call-start = ((), (), s32[]{:S(2)}) async-start(), calls=%async_computation.6 | async-start | bytes 146800640 | tf_op jit(solution)/shard_map/reduce_scatter | solution.py:19
  865.9 2021.9 %all-gather.5.cloned.1.call-start = ((), (), s32[]{:S(2)}) async-start(), calls=%async_computation.7 | async-start | bytes 146800640 | tf_op jit(solution)/shard_map/all_gather | solution.py:21
  2212.5 1301.9 %all-reduce.3.cloned.1.call-start = ((), (), s32[]{:S(2)}) async-start(), calls=%async_computation.8 | async-start | bytes 41943040
  3052.1 0.7 copy-start
  3538.0 120.8 %slice-start = ((s8[10485760]{0:T(1024)(128)(4,1)}), s8[4194304]{0:T(1024)(128)(4,1)S(1)}, s32[]{:S(2)}) async-start(s8[10485760]{0:T(1024)(128)(4,1)} %bitcast.24), calls=%async_computation.9 | async-start | bytes 8388608
  3538.0 120.8 %slice-start.1 = ((s8[10485760]{0:T(1024)(128)(4,1)}), s8[4194304]{0:T(1024)(128)(4,1)S(1)}, s32[]{:S(2)}) async-start(s8[10485760]{0:T(1024)(128)(4,1)} %bitcast.24), calls=%async_computation.10 | async-start | bytes 8388608
  3538.0 120.8 %slice-start.2 = ((s8[10485760]{0:T(1024)(128)(4,1)}), s8[2097152]{0:T(1024)(128)(4,1)S(1)}, s32[]{:S(2)}) async-start(s8[10485760]{0:T(1024)(128)(4,1)} %bitcast.24), calls=%async_computation.11 | async-start | bytes 4194304
Sparse Core Ops, SparseCore 0:
  21.1 247.7 all-gather.2
  701.5 738.6 reduce-scatter.5
  1442.8 739.7 reduce-scatter.7
  2212.6 675.1 all-gather.4
  3052.2 462.0 all-reduce.2
where the time goes:
time: 3690 us
  waiting for transfers between devices  2700 us (73%)
  matrix products  493 us (13%)
  blocking collectives  361 us (10%)
  local copies, waits for them, and re-layouts  81 us (2%)
  other arithmetic  37 us (1%)
    reduce_scatter x1, waiting for transfers between devices, body(): lax.psum_scatter(pb, 'dp', scatter_dimension=0, tiled=True)  742 us
    all_gather x1, waiting for transfers between devices, body(): hg = lax.all_gather(h, 'dp', axis=0, tiled=True)  675 us
    reduce_scatter x1, waiting for transfers between devices, body(): lax.psum_scatter(pa, 'dp', scatter_dimension=0, tiled=True)  574 us
    unnamed x6, waiting for transfers between devices  461 us
    all_gather x1, waiting for transfers between devices, body(): xt = lax.all_gather(x, 'tp', axis=0, tiled=True)  248 us
    all_to_all x1, blocking collectives, body(): xc = lax.all_to_all(xt, 'dp', 1, 0, tiled=True)  240 us
    dot_general x1, matrix products, body(): jnp.dot(hg, wd, preferred_element_type=jnp.float32).astype(jnp.bfloat16)  164 us
    dot_general x1, matrix products, body(): jnp.dot(xc, wu, preferred_element_type=jnp.float32).astype(jnp.bfloat16)  164 us
  transfers between devices with their start and end apart: 5, of which 5 were waited for; matrix products, arithmetic and copies ran while one was open for 4% of the time, Pallas kernels for 0%

commit v1 on v0

v1 whole, which is shorter than its diff:
```python
import jax
import jax.numpy as jnp
from jax import lax
from jax.sharding import PartitionSpec as P

COLS = 1792
STRIP = 256


def solution(mesh):
    nt = mesh.shape["tp"]
    nd = mesh.shape["dp"]
    swap = [(i, (i + 1) % nt) for i in range(nt)]

    def body(x, wg, wu, wd):
        r, d = x.shape
        f = wg.shape[1]
        dc = wd.shape[1]
        xc = jnp.concatenate([x, lax.ppermute(x, "tp", swap)], axis=0)
        hs = []
        for s in range(0, f, COLS):
            g = lax.all_gather(wg[:, s:s + COLS], "dp", axis=0, tiled=True)
            u = lax.all_gather(wu[:, s:s + COLS], "dp", axis=0, tiled=True)
            a = jnp.dot(xc, g, preferred_element_type=jnp.float32)
            b = jnp.dot(xc, u, preferred_element_type=jnp.float32)
            hs.append((jax.nn.silu(a) * b).astype(jnp.bfloat16))
        h = jnp.concatenate(hs, axis=1)
        outs = []
        for s in range(0, dc, STRIP):
            w = lax.all_gather(wd[:, s:s + STRIP], "dp", axis=0, tiled=False)
            p = [jnp.dot(h, w[i], preferred_element_type=jnp.float32).astype(jnp.bfloat16) for i in range(nd)]
            mine = jnp.stack([q[:r] for q in p])
            theirs = lax.ppermute(jnp.stack([q[r:] for q in p]), "tp", swap)
            outs.append(mine.astype(jnp.float32) + theirs.astype(jnp.float32))
        o = jnp.stack(outs)
        o = o.transpose(2, 1, 0, 3).reshape(r, d)
        return (x.astype(jnp.float32) + o).astype(jnp.bfloat16)

    return jax.shard_map(body, mesh=mesh, in_specs=(P(("dp", "tp"), None), P("dp", "tp"), P("dp", "tp"), P("tp", "dp")), out_specs=P(("dp", "tp"), None), check_vma=False)
```

time: 3690 us -> 1580 us (0.43)
  waiting for transfers between devices: 2700 us -> 702 us
  blocking collectives: 361 us -> 0 us
  matrix products: 493 us -> 688 us
    reduce_scatter x2 -> x0, waiting for transfers between devices: 1320 us -> none  [the longest x1 742 us: body(): lax.psum_scatter(pb, 'dp', scatter_dimension=0, tiled=True)]
    all_gather x2 -> x13, waiting for transfers between devices: 923 us -> 460 us  [the longest x4 265 us: body(): u = lax.all_gather(wu[:, s:s + COLS], 'dp', axis=0, tiled=True)]
    unnamed x6 -> x13, waiting for transfers between devices: 461 us -> 5.62 us
    all_to_all x2 -> x0, blocking collectives: 361 us -> none  [the longest x1 240 us: body(): xc = lax.all_to_all(xt, 'dp', 1, 0, tiled=True)]
    ppermute x0 -> x6, waiting for transfers between devices: none -> 237 us  [the longest x1 217 us: body(): xc = jnp.concatenate([x, lax.ppermute(x, 'tp', swap)], axis=0)]
    dot_general x3 -> x28, matrix products: 493 us -> 688 us  [the longest x20 290 us: body(): jnp.dot(h, w[i], preferred_element_type=jnp.float32).astype(jnp.bfloat16)]
    slice x0 -> x3, local copies, waits for them, and re-layouts: none -> 41.1 us  [the longest x1 13.9 us: body(): g = lax.all_gather(wg[:, s:s + COLS], 'dp', axis=0, tiled=True)]
  transfers between devices with their start and end apart: 5 -> 19, of which waited for: 5 -> 12; matrix products, arithmetic and copies ran while one was open for 4% -> 51% of each run, Pallas kernels for 0% -> 0%
where the time goes in v1:
time: 1580 us
  waiting for transfers between devices  702 us (44%)
  matrix products  688 us (44%)
  local copies, waits for them, and re-layouts  115 us (7%)
  other arithmetic  48.5 us (3%)
    dot_general x20, matrix products, body(): jnp.dot(h, w[i], preferred_element_type=jnp.float32).astype(jnp.bfloat16)  290 us
    all_gather x4, waiting for transfers between devices, body(): u = lax.all_gather(wu[:, s:s + COLS], 'dp', axis=0, tiled=True)  265 us
    ppermute x1, waiting for transfers between devices, body(): xc = jnp.concatenate([x, lax.ppermute(x, 'tp', swap)], axis=0)  217 us
    dot_general x4, matrix products, body(): b = jnp.dot(xc, u, preferred_element_type=jnp.float32)  205 us
    dot_general x4, matrix products, body(): a = jnp.dot(xc, g, preferred_element_type=jnp.float32)  193 us
    all_gather x5, waiting for transfers between devices, body(): w = lax.all_gather(wd[:, s:s + STRIP], 'dp', axis=0, tiled=False)  143 us
    all_gather x4, waiting for transfers between devices, body(): g = lax.all_gather(wg[:, s:s + COLS], 'dp', axis=0, tiled=True)  52.4 us
  transfers between devices with their start and end apart: 19, of which 12 were waited for; matrix products, arithmetic and copies ran while one was open for 51% of the time, Pallas kernels for 0%

profile of v1, /device:TPU:0, one launch (start us, length us, event | category | flops | bytes accessed | tf_op | source)
XLA Modules:
  0.0 1579.2 jit_solution(6629283810286591855)
XLA Ops:
  6.5 13.9 fusion.102
  22.6 13.9 fusion.103
  38.6 13.3 fusion.101
  57.5 8.7 constant_dynamic-update-slice_fusion.1
  66.2 216.7 %collective-permute-done = bf16[1024,5120]{1,0:T(8,128)(2,1)} collective-permute-done((bf16[1024,5120]{1,0:T(8,128)(2,1)}, bf16[1024,5120]{1,0:T(8,128)(2,1)}, u32[]{:S(2)}, u32[]{:S(2)}) %collective-permute-start) | collective-permute-done | bytes 10485792 | tf_op jit(solution)/shard_map/ppermute | solution.py:19
  291.4 48.0 %fusion.104 = f32[2048,1792]{0,1:T(8,128)} fusion(bf16[2048,5120]{1,0:T(8,128)(2,1)} %constant_dynamic-update-slice_fusion, bf16[5120,1792]{1,0:T(8,128)(2,1)} %all-gather.19.cloned.1.call-done), kind=kOutput, calls=%fused_computation.122 | convolution fusion | flops 37580963840 | bytes 54001664 | tf_op jit(solution)/shard_map/dot_general | solution.py:24
  339.4 48.3 %fusion.105 = f32[2048,1792]{0,1:T(8,128)} fusion(bf16[2048,5120]{1,0:T(8,128)(2,1)} %constant_dynamic-update-slice_fusion, bf16[5120,1792]{1,0:T(8,128)(2,1)} %all-gather.23.cloned.1.call-done), kind=kOutput, calls=%fused_computation.123 | convolution fusion | flops 37580963840 | bytes 54001664 | tf_op jit(solution)/shard_map/dot_general | solution.py:24
  387.7 48.5 %fusion.106 = f32[2048,1792]{0,1:T(8,128)} fusion(bf16[2048,5120]{1,0:T(8,128)(2,1)} %constant_dynamic-update-slice_fusion, bf16[5120,1792]{1,0:T(8,128)(2,1)} %all-gather.27.cloned.1.call-done), kind=kOutput, calls=%fused_computation.124 | convolution fusion | flops 37580963840 | bytes 54001664 | tf_op jit(solution)/shard_map/dot_general | solution.py:24
  436.2 52.4 %all-gather.31.cloned.1.call-done = bf16[5120,1792]{1,0:T(8,128)(2,1)} async-done(((bf16[1280,1792]{1,0:T(8,128)(2,1)}), bf16[5120,1792]{1,0:T(8,128)(2,1)}) %all-gather.31.cloned.1.call-update) | async-done | bytes 18350096 | tf_op jit(solution)/shard_map/all_gather | solution.py:22
  488.6 48.3 %fusion.107 = f32[2048,1792]{0,1:T(8,128)} fusion(bf16[2048,5120]{1,0:T(8,128)(2,1)} %constant_dynamic-update-slice_fusion, bf16[5120,1792]{1,0:T(8,128)(2,1)} %all-gather.31.cloned.1.call-done), kind=kOutput, calls=%fused_computation.125 | convolution fusion | flops 37580963840 | bytes 54001664 | tf_op jit(solution)/shard_map/dot_general | solution.py:24
  537.0 68.3 %all-gather.21.cloned.1.call-done = bf16[5120,1792]{1,0:T(8,128)(2,1)} async-done(((bf16[1280,1792]{1,0:T(8,128)(2,1)}), bf16[5120,1792]{1,0:T(8,128)(2,1)}) %all-gather.21.cloned.1.call-update) | async-done | bytes 18350096 | tf_op jit(solution)/shard_map/all_gather | solution.py:23
  605.2 51.1 %multiply_convert_fusion.3 = bf16[2048,1792]{0,1:T(8,128)(2,1)} fusion(f32[2048,1792]{0,1:T(8,128)} %fusion.104, bf16[2048,5120]{1,0:T(8,128)(2,1)} %constant_dynamic-update-slice_fusion, bf16[5120,1792]{1,0:T(8,128)(2,1)} %all-gather.21.cloned.1.call-done), kind=kOutput, calls=%fused_computation.6 | convolution fusion | flops 37602983936 | bytes 61341696 | tf_op jit(solution)/shard_map/dot_general | solution.py:25
  656.4 65.4 %all-gather.25.cloned.1.call-done = bf16[5120,1792]{1,0:T(8,128)(2,1)} async-done(((bf16[1280,1792]{1,0:T(8,128)(2,1)}), bf16[5120,1792]{1,0:T(8,128)(2,1)}) %all-gather.25.cloned.1.call-update) | async-done | bytes 18350096 | tf_op jit(solution)/shard_map/all_gather | solution.py:23
  721.8 51.2 %multiply_convert_fusion.2 = bf16[2048,1792]{0,1:T(8,128)(2,1)} fusion(f32[2048,1792]{0,1:T(8,128)} %fusion.105, bf16[2048,5120]{1,0:T(8,128)(2,1)} %constant_dynamic-update-slice_fusion, bf16[5120,1792]{1,0:T(8,128)(2,1)} %all-gather.25.cloned.1.call-done), kind=kOutput, calls=%fused_computation.5 | convolution fusion | flops 37602983936 | bytes 61341696 | tf_op jit(solution)/shard_map/dot_general | solution.py:25
  773.0 65.5 %all-gather.29.cloned.1.call-done = bf16[5120,1792]{1,0:T(8,128)(2,1)} async-done(((bf16[1280,1792]{1,0:T(8,128)(2,1)}), bf16[5120,1792]{1,0:T(8,128)(2,1)}) %all-gather.29.cloned.1.call-update) | async-done | bytes 18350096 | tf_op jit(solution)/shard_map/all_gather | solution.py:23
  838.5 51.4 %multiply_convert_fusion.1 = bf16[2048,1792]{0,1:T(8,128)(2,1)} fusion(f32[2048,1792]{0,1:T(8,128)} %fusion.106, bf16[2048,5120]{1,0:T(8,128)(2,1)} %constant_dynamic-update-slice_fusion, bf16[5120,1792]{1,0:T(8,128)(2,1)} %all-gather.29.cloned.1.call-done), kind=kOutput, calls=%fused_computation.4 | convolution fusion | flops 37602983936 | bytes 61341696 | tf_op jit(solution)/shard_map/dot_general | solution.py:25
  889.9 65.3 %all-gather.33.cloned.1.call-done = bf16[5120,1792]{1,0:T(8,128)(2,1)} async-done(((bf16[1280,1792]{1,0:T(8,128)(2,1)}), bf16[5120,1792]{1,0:T(8,128)(2,1)}) %all-gather.33.cloned.1.call-update) | async-done | bytes 18350096 | tf_op jit(solution)/shard_map/all_gather | solution.py:23
  955.3 51.1 %multiply_convert_fusion = bf16[2048,1792]{0,1:T(8,128)(2,1)} fusion(f32[2048,1792]{0,1:T(8,128)} %fusion.107, bf16[2048,5120]{1,0:T(8,128)(2,1)} %constant_dynamic-update-slice_fusion, bf16[5120,1792]{1,0:T(8,128)(2,1)} %all-gather.33.cloned.1.call-done), kind=kOutput, calls=%fused_computation.3 | convolution fusion | flops 37602983936 | bytes 61341696 | tf_op jit(solution)/shard_map/dot_general | solution.py:25
  1006.3 21.2 %pad_maximum_fusion = bf16[2048,7168]{0,1:T(8,128)(2,1)} fusion(bf16[2048,1792]{0,1:T(8,128)(2,1)} %multiply_convert_fusion, bf16[2048,1792]{0,1:T(8,128)(2,1)} %multiply_convert_fusion.1, bf16[2048,1792]{0,1:T(8,128)(2,1)} %multiply_convert_fusion.2, bf16[2048,1792]{0,1:T(8,128)(2,1)} %multiply_convert_fusion.3), kind=kLoop, calls=%fused_computation | loop fusion | flops 117440512 | bytes 58720256 | tf_op jit(solution)/shard_map/concatenate | solution.py:27
  1027.5 21.4 %all-gather.41.cloned.1.call-done = bf16[28672,256]{1,0:T(8,128)(2,1)} async-done(((bf16[7168,256]{1,0:T(8,128)(2,1)}), bf16[28672,256]{1,0:T(8,128)(2,1)}) %all-gather.41.cloned.1.call-update) | async-done | bytes 14680080 | tf_op jit(solution)/shard_map/all_gather | solution.py:30
  1048.9 14.4 fusion.77
  1063.3 14.6 fusion.80
  1079.2 14.4 fusion.83
  1093.6 14.8 fusion.86
  1112.8 29.6 %all-gather.39.cloned.1.call-done = bf16[28672,256]{1,0:T(8,128)(2,1)} async-done(((bf16[7168,256]{1,0:T(8,128)(2,1)}), bf16[28672,256]{1,0:T(8,128)(2,1)}) %all-gather.39.cloned.1.call-update) | async-done | bytes 14680080 | tf_op jit(solution)/shard_map/all_gather | solution.py:30
  1142.4 14.4 fusion.65
  1156.8 14.4 fusion.68
  1172.4 14.6 fusion.71
  1187.0 14.4 fusion.74
  1205.6 30.4 %all-gather.37.cloned.1.call-done = bf16[28672,256]{1,0:T(8,128)(2,1)} async-done(((bf16[7168,256]{1,0:T(8,128)(2,1)}), bf16[28672,256]{1,0:T(8,128)(2,1)}) %all-gather.37.cloned.1.call-update) | async-done | bytes 14680080 | tf_op jit(solution)/shard_map/all_gather | solution.py:30
  1236.0 14.6 fusion.53
  1250.6 14.4 fusion.56
  1266.3 14.4 fusion.59
  1280.7 14.8 fusion.62
  1298.5 31.0 %all-gather.35.cloned.1.call-done = bf16[28672,256]{1,0:T(8,128)(2,1)} async-done(((bf16[7168,256]{1,0:T(8,128)(2,1)}), bf16[28672,256]{1,0:T(8,128)(2,1)}) %all-gather.35.cloned.1.call-update) | async-done | bytes 14680080 | tf_op jit(solution)/shard_map/all_gather | solution.py:30
  1329.5 14.4 fusion.41
  1343.9 14.4 fusion.44
  1359.5 14.6 fusion.47
  1374.1 14.4 fusion.50
  1392.9 30.2 %all-gather.43.cloned.1.call-done = bf16[28672,256]{1,0:T(8,128)(2,1)} async-done(((bf16[7168,256]{1,0:T(8,128)(2,1)}), bf16[28672,256]{1,0:T(8,128)(2,1)}) %all-gather.43.cloned.1.call-update) | async-done | bytes 14680080 | tf_op jit(solution)/shard_map/all_gather | solution.py:30
  1423.1 14.6 fusion.89
  1437.7 14.4 fusion.92
  1452.2 14.4 fusion.95
  1466.6 14.7 fusion.98
  1486.6 14.4 copy.5
  1512.6 20.4 %collective-permute-done.5 = bf16[4,1024,256]{1,2,0:T(8,128)(2,1)} collective-permute-done((bf16[4,1024,256]{1,2,0:T(8,128)(2,1)}, bf16[4,1024,256]{1,2,0:T(8,128)(2,1)}, u32[]{:S(2)}, u32[]{:S(2)}) %collective-permute-start.5) | collective-permute-done | bytes 2097184 | tf_op jit(solution)/shard_map/ppermute | solution.py:33
  1542.6 9.6 copy.6
  1558.7 13.7 copy.7
  (94 shorter events, 71.9 us)
Async XLA Ops:
  6.5 284.9 %all-gather.19.cloned.1.call-start = ((), (), s32[]{:S(2)}) async-start(), calls=%async_computation | async-start | bytes 22937600 | tf_op jit(solution)/shard_map/all_gather | solution.py:22
  20.5 319.0 %all-gather.23.cloned.1.call-start = ((), (), s32[]{:S(2)}) async-start(), calls=%async_computation.2 | async-start | bytes 22937600 | tf_op jit(solution)/shard_map/all_gather | solution.py:22
  21.2 366.5 %all-gather.27.cloned.1.call-start = ((), (), s32[]{:S(2)}) async-start(), calls=%async_computation.4 | async-start | bytes 22937600 | tf_op jit(solution)/shard_map/all_gather | solution.py:22
  21.9 466.7 %all-gather.31.cloned.1.call-start = ((), (), s32[]{:S(2)}) async-start(), calls=%async_computation.6 | async-start | bytes 22937600 | tf_op jit(solution)/shard_map/all_gather | solution.py:22
  22.5 582.7 %all-gather.21.cloned.1.call-start = ((), (), s32[]{:S(2)}) async-start(), calls=%async_computation.1 | async-start | bytes 22937600 | tf_op jit(solution)/shard_map/all_gather | solution.py:23
  36.5 685.3 %all-gather.25.cloned.1.call-start = ((), (), s32[]{:S(2)}) async-start(), calls=%async_computation.3 | async-start | bytes 22937600 | tf_op jit(solution)/shard_map/all_gather | solution.py:23
  37.1 801.5 %all-gather.29.cloned.1.call-start = ((), (), s32[]{:S(2)}) async-start(), calls=%async_computation.5 | async-start | bytes 22937600 | tf_op jit(solution)/shard_map/all_gather | solution.py:23
  37.8 917.5 %all-gather.33.cloned.1.call-start = ((), (), s32[]{:S(2)}) async-start(), calls=%async_computation.7 | async-start | bytes 22937600 | tf_op jit(solution)/shard_map/all_gather | solution.py:23
  38.6 1010.3 %all-gather.41.cloned.1.call-start = ((), (), s32[]{:S(2)}) async-start(), calls=%async_computation.11 | async-start | bytes 18350080 | tf_op jit(solution)/shard_map/all_gather | solution.py:30
  51.9 1090.4 %all-gather.39.cloned.1.call-start = ((), (), s32[]{:S(2)}) async-start(), calls=%async_computation.10 | async-start | bytes 18350080 | tf_op jit(solution)/shard_map/all_gather | solution.py:30
  52.5 1183.5 %all-gather.37.cloned.1.call-start = ((), (), s32[]{:S(2)}) async-start(), calls=%async_computation.9 | async-start | bytes 18350080 | tf_op jit(solution)/shard_map/all_gather | solution.py:30
  53.2 1276.3 %all-gather.35.cloned.1.call-start = ((), (), s32[]{:S(2)}) async-start(), calls=%async_computation.8 | async-start | bytes 18350080 | tf_op jit(solution)/shard_map/all_gather | solution.py:30
  53.8 1369.3 %all-gather.43.cloned.1.call-start = ((), (), s32[]{:S(2)}) async-start(), calls=%async_computation.12 | async-start | bytes 18350080 | tf_op jit(solution)/shard_map/all_gather | solution.py:30
  54.0 228.8 %collective-permute-start = (bf16[1024,5120]{1,0:T(8,128)(2,1)}, bf16[1024,5120]{1,0:T(8,128)(2,1)}, u32[]{:S(2)}, u32[]{:S(2)}) collective-permute-start(bf16[1024,5120]{1,0:T(8,128)(2,1)} %param.4), channel_id=1, source_target_pairs={{0,4},{4,0},{1,5},{5,1},{2,6},{6,2},{3,7},{7,3}} | collective-permute-start | bytes 31457288 | tf_op jit(solution)/shard_map/ppermute | solution.py:19
  1111.3 398.7 %collective-permute-start.4 = (bf16[4,1024,256]{1,2,0:T(8,128)(2,1)}, bf16[4,1024,256]{1,2,0:T(8,128)(2,1)}, u32[]{:S(2)}, u32[]{:S(2)}) collective-permute-start(bf16[4,1024,256]{1,2,0:T(8,128)(2,1)} %pad_maximum_fusion.4), channel_id=1, source_target_pairs={{0,4},{4,0},{1,5},{5,1},{2,6},{6,2},{3,7},{7,3}} | collective-permute-start | bytes 6291464 | tf_op jit(solution)/shard_map/ppermute | solution.py:33
  1204.1 303.4 %collective-permute-start.3 = (bf16[4,1024,256]{1,2,0:T(8,128)(2,1)}, bf16[4,1024,256]{1,2,0:T(8,128)(2,1)}, u32[]{:S(2)}, u32[]{:S(2)}) collective-permute-start(bf16[4,1024,256]{1,2,0:T(8,128)(2,1)} %pad_maximum_fusion.3), channel_id=1, source_target_pairs={{0,4},{4,0},{1,5},{5,1},{2,6},{6,2},{3,7},{7,3}} | collective-permute-start | bytes 6291464 | tf_op jit(solution)/shard_map/ppermute | solution.py:33
  1297.0 207.4 %collective-permute-start.2 = (bf16[4,1024,256]{1,2,0:T(8,128)(2,1)S(1)}, bf16[4,1024,256]{1,2,0:T(8,128)(2,1)}, u32[]{:S(2)}, u32[]{:S(2)}) collective-permute-start(bf16[4,1024,256]{1,2,0:T(8,128)(2,1)S(1)} %pad_maximum_fusion.2), channel_id=1, source_target_pairs={{0,4},{4,0},{1,5},{5,1},{2,6},{6,2},{3,7},{7,3}} | collective-permute-start | bytes 6291464 | tf_op jit(solution)/shard_map/ppermute | solution.py:33
  1391.4 109.6 %collective-permute-start.1 = (bf16[4,1024,256]{1,2,0:T(8,128)(2,1)}, bf16[4,1024,256]{1,2,0:T(8,128)(2,1)}, u32[]{:S(2)}, u32[]{:S(2)}) collective-permute-start(bf16[4,1024,256]{1,2,0:T(8,128)(2,1)} %pad_maximum_fusion.1), channel_id=1, source_target_pairs={{0,4},{4,0},{1,5},{5,1},{2,6},{6,2},{3,7},{7,3}} | collective-permute-start | bytes 6291464 | tf_op jit(solution)/shard_map/ppermute | solution.py:33
  1485.2 22.4 %copy-start.5 = (bf16[1,1024,256]{1,2,0:T(8,128)(2,1)S(1)}, bf16[1,1024,256]{1,2,0:T(8,128)(2,1)}, u32[]{:S(2)}) copy-start(bf16[1,1024,256]{1,2,0:T(8,128)(2,1)} %get-tuple-element.36) | copy-start | bytes 1572868
  1485.2 22.4 %copy-start.6 = (bf16[1,1024,256]{1,2,0:T(8,128)(2,1)S(1)}, bf16[1,1024,256]{1,2,0:T(8,128)(2,1)}, u32[]{:S(2)}) copy-start(bf16[1,1024,256]{1,2,0:T(8,128)(2,1)} %get-tuple-element.69) | copy-start | bytes 1572868
  1485.2 47.8 %collective-permute-start.5 = (bf16[4,1024,256]{1,2,0:T(8,128)(2,1)}, bf16[4,1024,256]{1,2,0:T(8,128)(2,1)}, u32[]{:S(2)}, u32[]{:S(2)}) collective-permute-start(bf16[4,1024,256]{1,2,0:T(8,128)(2,1)} %pad_maximum_fusion.5), channel_id=1, source_target_pairs={{0,4},{4,0},{1,5},{5,1},{2,6},{6,2},{3,7},{7,3}} | collective-permute-start | bytes 6291464 | tf_op jit(solution)/shard_map/ppermute | solution.py:33
  1501.0 6.6 copy-start.7
  1501.0 6.6 copy-start.8
  1501.0 9.1 copy-start.1
  1501.0 9.1 copy-start.2
  1501.0 9.1 copy-start.3
  1501.0 9.1 copy-start.4
  1504.3 28.7 %copy-start.9 = (bf16[1,1024,256]{1,2,0:T(8,128)(2,1)S(1)}, bf16[1,1024,256]{1,2,0:T(8,128)(2,1)}, u32[]{:S(2)}) copy-start(bf16[1,1024,256]{1,2,0:T(8,128)(2,1)} %get-tuple-element.20) | copy-start | bytes 1572868
  1504.3 28.6 %copy-start.10 = (bf16[1,1024,256]{1,2,0:T(8,128)(2,1)S(1)}, bf16[1,1024,256]{1,2,0:T(8,128)(2,1)}, u32[]{:S(2)}) copy-start(bf16[1,1024,256]{1,2,0:T(8,128)(2,1)} %get-tuple-element.77) | copy-start | bytes 1572868
  1504.3 28.6 %copy-start.11 = (bf16[1,1024,256]{1,2,0:T(8,128)(2,1)S(1)}, bf16[1,1024,256]{1,2,0:T(8,128)(2,1)}, u32[]{:S(2)}) copy-start(bf16[1,1024,256]{1,2,0:T(8,128)(2,1)} %get-tuple-element.24) | copy-start | bytes 1572868
  1504.3 28.6 %copy-start.12 = (bf16[1,1024,256]{1,2,0:T(8,128)(2,1)S(1)}, bf16[1,1024,256]{1,2,0:T(8,128)(2,1)}, u32[]{:S(2)}) copy-start(bf16[1,1024,256]{1,2,0:T(8,128)(2,1)} %get-tuple-element.75) | copy-start | bytes 1572868
  1533.0 19.2 %slice-start = ((s8[10485760]{0:T(1024)(128)(4,1)}), s8[4194304]{0:T(1024)(128)(4,1)S(1)}, s32[]{:S(2)}) async-start(s8[10485760]{0:T(1024)(128)(4,1)} %bitcast.131), calls=%async_computation.13 | async-start | bytes 8388608
  1535.6 7.0 copy-start
  1542.6 9.6 slice-start.1
  1542.6 9.6 slice-start.2
Sparse Core Ops, SparseCore 0:
  20.6 117.9 all-gather.18
  140.1 115.1 all-gather.22
  256.9 115.1 all-gather.26
  373.5 115.1 all-gather.30
  490.0 115.1 all-gather.20
  606.6 115.1 all-gather.24
  723.3 115.1 all-gather.28
  840.1 115.1 all-gather.32
  956.8 92.0 all-gather.40
  1050.3 92.0 all-gather.38
  1143.9 92.0 all-gather.36
  1237.4 92.0 all-gather.34
  1331.0 92.0 all-gather.42

commit v2 on v0

v2 whole, which is shorter than its diff:
```python
import functools

import jax
import jax.numpy as jnp
from jax import lax
from jax.experimental import pallas as pl
from jax.experimental.pallas import tpu as pltpu
from jax.sharding import PartitionSpec as P

CW = 256


def kernel(x, wg, wu, wd, y, w1, w2, w3, db, hb, po, rdi, r1i, yxi,
           xb, wv, hst, s_loc, s_xs, s_ws, s_xx, s_xy, s_xd, s_w1, s_w2, s_w3, s_d1, s_d2, s_d3,
           s_wv, s_h, s_po, s_rs, s_rd, s_r1, s_yx, s_ys, s_ld, s_out):
    rows, dim = x.shape
    dk = dim // 4
    fq = wg.shape[1] // 2
    nch = fq // CW
    first = nch // 2
    ns = dk // CW
    f32, bf16 = jnp.float32, jnp.bfloat16

    t = lax.axis_index("tp")
    d = lax.axis_index("dp")
    side = d // 2
    core = d % 2
    mate = d + 1 - 2 * core
    quarter = [d, mate, (d + 2) % 4, (mate + 2) % 4]
    to_mate = {"dp": mate}
    to_x = {"dp": (d + 2) % 4}
    to_y = {"tp": 1 - t}

    def col(v, size=128):
        return pl.multiple_of(v, size)

    def send(src, dst, send_sem, recv_sem, where):
        pltpu.make_async_remote_copy(
            src_ref=src, dst_ref=dst, send_sem=send_sem, recv_sem=recv_sem,
            device_id=where, device_id_type=pl.DeviceIdType.MESH).start()

    def wait(ref, sem):
        pltpu.make_async_copy(ref, ref, sem).wait()

    def block(b):
        return pl.ds(b * rows, rows)

    def slot(s):
        return pl.ds(s * dk, dk)

    barrier = pltpu.get_barrier_semaphore()
    for where in (to_mate, to_x, to_y):
        pl.semaphore_signal(barrier, inc=1, device_id=where, device_id_type=pl.DeviceIdType.MESH)
    pl.semaphore_wait(barrier, 3)

    for s in range(4):
        src = x.at[:, pl.ds(col(quarter[s] * dk), dk)]
        send(src, xb.at[block(2), slot(s ^ 2)], s_xs.at[0], s_xx.at[s ^ 2], to_x)
        send(src, xb.at[block(1), slot(s)], s_xs.at[1], s_xy.at[s], to_y)
    for s in range(4):
        src = x.at[:, pl.ds(col(quarter[s] * dk), dk)]
        pltpu.make_async_copy(src, xb.at[block(0), slot(s)], s_loc).start()

    def send_chunk(j, _):
        for m, w in enumerate((wg, wu)):
            away = w.at[:, pl.ds(col((1 - side) * fq + j * CW), CW)]
            here = w.at[:, pl.ds(col(side * fq + j * CW), CW)]
            send(away, w2.at[j, :, pl.ds(m * CW, CW)], s_ws.at[1], s_w2.at[j], to_x)
            send(here, w1.at[j, :, pl.ds(m * CW, CW)], s_ws.at[0], s_w1.at[j], to_mate)
        return 0

    lax.fori_loop(0, nch, send_chunk, 0)

    def send_strip(k, _):
        cols = pl.ds(col(k * CW), CW)
        send(wd.at[pl.ds(col((1 - side) * fq), fq), cols], db.at[1, k], s_ws.at[3], s_d2.at[k], to_x)
        send(wd.at[pl.ds(col(side * fq), fq), cols], db.at[0, k], s_ws.at[2], s_d1.at[k], to_mate)
        return 0

    lax.fori_loop(0, ns, send_strip, 0)

    for s in (2, 3, 0, 1):
        piece = xb.at[block(2), slot(s)]
        wait(piece, s_xx.at[s])
        send(piece, xb.at[block(3), slot(s)], s_xs.at[2], s_xd.at[s], to_y)

    def forward_chunk(j):
        wait(w2.at[j], s_w2.at[j])
        send(w2.at[j], w3.at[j], s_ws.at[4], s_w3.at[j], to_mate)

    def load_chunk(j, p):
        for m, w in enumerate((wg, wu)):
            here = w.at[:, pl.ds(col(side * fq + j * CW), CW)]
            pltpu.make_async_copy(here, wv.at[p, slot(0), pl.ds(m * CW, CW)], s_wv.at[p]).start()
        for s, w in ((1, w1), (2, w2), (3, w3)):
            pltpu.make_async_copy(w.at[j], wv.at[p, slot(s)], s_wv.at[p]).start()

    def arrive_chunk(j):
        wait(w1.at[j], s_w1.at[j])
        wait(w3.at[j], s_w3.at[j])

    def hcopy(b, j, q):
        return pltpu.make_async_copy(
            hst.at[q], hb.at[block(b), pl.ds(col(j * CW), CW)], s_h.at[q])

    def gate(b, j, p, q, used=True):
        ab = jnp.dot(xb[block(b), :], wv[p], preferred_element_type=f32)
        a = ab[:, :CW]
        h = (a * jax.nn.sigmoid(a) * ab[:, CW:]).astype(bf16)

        @pl.when(used)
        def _():
            hcopy(b, j, q).wait()

        hst[q] = h
        hcopy(b, j, q).start()

    forward_chunk(0)
    arrive_chunk(0)
    load_chunk(0, 0)
    wait(xb.at[block(0), :], s_loc)
    for s in range(4):
        wait(xb.at[block(1), slot(s)], s_xy.at[s])

    def pass_one(j, _):
        p = j % 2
        wait(wv.at[p], s_wv.at[p])
        gate(0, j, p, 0, j > 0)
        gate(1, j, p, 1, j > 0)

        @pl.when(j + 1 < first)
        def _():
            forward_chunk(j + 1)

        gate(2, j, p, 0)

        @pl.when(j + 1 < first)
        def _():
            arrive_chunk(j + 1)
            load_chunk(j + 1, 1 - p)

        return 0

    lax.fori_loop(0, first, pass_one, 0)

    load_chunk(0, 0)
    for s in range(4):
        wait(xb.at[block(3), slot(s)], s_xd.at[s])

    def pass_diag(j, _):
        p = j % 2

        @pl.when(j + 1 < first)
        def _():
            load_chunk(j + 1, 1 - p)

        wait(wv.at[p], s_wv.at[p])
        gate(3, j, p, 1)
        return 0

    lax.fori_loop(0, first, pass_diag, 0)

    forward_chunk(first)
    arrive_chunk(first)
    load_chunk(first, first % 2)

    def pass_two(j, _):
        p = j % 2
        wait(wv.at[p], s_wv.at[p])
        gate(3, j, p, 0)
        gate(1, j, p, 1)

        @pl.when(j + 1 < nch)
        def _():
            forward_chunk(j + 1)

        gate(2, j, p, 0)

        @pl.when(j + 1 < nch)
        def _():
            arrive_chunk(j + 1)
            load_chunk(j + 1, 1 - p)

        gate(0, j, p, 1)
        return 0

    lax.fori_loop(first, nch, pass_two, 0)
    for q in range(2):
        hcopy(0, 0, q).wait()

    wait(xb.at[block(2), :], s_xs.at[2])
    hcols = pl.ds(0, fq)
    for b in (3, 1, 2, 0):
        pltpu.make_async_copy(hb.at[block(b), :], xb.at[block(b), hcols], s_ld.at[b]).start()

    def tile(b, c):
        return xb.at[block(b), pl.ds(col(fq + c * CW), CW)]

    def strip_slot(i):
        late = i - 2 * ns
        return (jnp.where(i < 2 * ns, i // ns, 2 + late % 2),
                jnp.where(i < 2 * ns, i % ns, late // 2))

    def load_strip(i, p):
        dst = wv.at[p, pl.ds(0, fq), pl.ds(0, CW)]
        late = i - 2 * ns

        @pl.when(i < ns)
        def _():
            src = wd.at[pl.ds(col(side * fq), fq), pl.ds(col(i * CW), CW)]
            pltpu.make_async_copy(src, dst, s_wv.at[p]).start()

        @pl.when((i >= ns) & (i < 2 * ns))
        def _():
            k = i - ns
            wait(db.at[0, k], s_d1.at[k])
            pltpu.make_async_copy(db.at[0, k], dst, s_wv.at[p]).start()

        @pl.when((i >= 2 * ns) & (late % 2 == 0))
        def _():
            k = late // 2
            wait(db.at[1, k], s_d2.at[k])
            send(db.at[1, k], db.at[2, k], s_ws.at[5], s_d3.at[k], to_mate)
            pltpu.make_async_copy(db.at[1, k], dst, s_wv.at[p]).start()

        @pl.when((i >= 2 * ns) & (late % 2 == 1))
        def _():
            k = late // 2
            wait(db.at[2, k], s_d3.at[k])
            pltpu.make_async_copy(db.at[2, k], dst, s_wv.at[p]).start()

    def put(b, i, p):
        return pltpu.make_async_copy(tile(b, p), po.at[b, i], s_po.at[b])

    def down(b, i, p):
        strip = wv[p, pl.ds(0, fq), pl.ds(0, CW)]
        o = jnp.dot(xb[block(b), hcols], strip, preferred_element_type=f32)
        xb[block(b), pl.ds(col(fq + p * CW), CW)] = o.astype(bf16)
        put(b, i, p).start()

    load_strip(0, 0)
    for b in (3, 1, 2, 0):
        wait(xb.at[block(b), hcols], s_ld.at[b])

    def partial(i, _):
        p = i % 2
        wait(wv.at[p, pl.ds(0, fq), pl.ds(0, CW)], s_wv.at[p])
        down(3, i, p)
        down(1, i, p)
        put(3, i, p).wait()
        send(po.at[3, i], rdi.at[i], s_rs.at[0], s_rd.at[i], to_y)

        @pl.when(i + 1 < 4 * ns)
        def _():
            load_strip(i + 1, 1 - p)

        down(2, i, p)
        put(1, i, p).wait()
        send(po.at[1, i], r1i.at[i], s_rs.at[1], s_r1.at[i], to_y)
        down(0, i, p)
        put(2, i, p).wait()
        put(0, i, p).wait()
        return 0

    lax.fori_loop(0, 4 * ns, partial, 0)

    def relay(i):
        q = i % 2
        pltpu.make_async_copy(po.at[2, i], tile(0, 0), s_ld.at[0]).start()
        wait(rdi.at[i], s_rd.at[i])
        pltpu.make_async_copy(rdi.at[i], tile(0, 1), s_ld.at[1]).start()
        wait(tile(0, 0), s_ld.at[0])
        wait(tile(0, 1), s_ld.at[1])

        @pl.when(i >= 2)
        def _():
            wait(tile(1, q), s_ys.at[q])

        o = xb[block(0), pl.ds(fq, CW)].astype(f32) + xb[block(0), pl.ds(fq + CW, CW)].astype(f32)
        xb[block(1), pl.ds(col(fq + q * CW), CW)] = o.astype(bf16)
        s, k = strip_slot(i)
        there = jnp.where(s < 2, 2 * ns + 2 * k + s, (s - 2) * ns + k)
        send(tile(1, q), yxi.at[there], s_ys.at[q], s_yx.at[there], to_x)

    def place(s, k):
        q = jnp.where(s == 0, quarter[0], jnp.where(s == 1, quarter[1], jnp.where(s == 2, quarter[2], quarter[3])))
        return pl.ds(col(q * dk + k * CW), CW)

    def finish(i, q, used):
        s, k = strip_slot(i)
        cols = place(s, k)
        pltpu.make_async_copy(po.at[0, i], tile(2, 0), s_ld.at[0]).start()
        pltpu.make_async_copy(x.at[:, cols], tile(2, 1), s_ld.at[1]).start()
        wait(r1i.at[i], s_r1.at[i])
        pltpu.make_async_copy(r1i.at[i], tile(2, 2), s_ld.at[2]).start()
        wait(yxi.at[i], s_yx.at[i])
        pltpu.make_async_copy(yxi.at[i], tile(2, 3), s_ld.at[3]).start()
        for c in range(4):
            wait(tile(2, c), s_ld.at[c])
        o = xb[block(2), pl.ds(fq, CW)].astype(f32)
        for c in range(1, 4):
            o = o + xb[block(2), pl.ds(fq + c * CW, CW)].astype(f32)
        out = pltpu.make_async_copy(tile(3, q), y.at[:, cols], s_out.at[q])

        @pl.when(used)
        def _():
            out.wait()

        xb[block(3), pl.ds(fq + q * CW, CW)] = o.astype(bf16)
        out.start()

    def tail(n, _):
        @pl.when(n < 4 * ns)
        def _():
            relay(n)

        @pl.when(n > 2 * ns)
        def _():
            m = n - 1
            late = m - 2 * ns
            finish(m, 0, late > 0)
            finish((late % 2) * ns + late // 2, 1, late > 0)

        return 0

    lax.fori_loop(0, 4 * ns + 1, tail, 0)

    for q in range(2):
        wait(tile(3, q), s_out.at[q])
        wait(tile(1, q), s_ys.at[q])
    wait(x, s_xs.at[0])
    wait(x, s_xs.at[1])
    wait(w1, s_ws.at[0])
    wait(w2, s_ws.at[1])
    wait(db.at[0], s_ws.at[2])
    wait(db.at[1], s_ws.at[3])
    wait(w3, s_ws.at[4])
    wait(db.at[2], s_ws.at[5])
    wait(rdi, s_rs.at[0])
    wait(r1i, s_rs.at[1])


def solution(mesh):
    def body(x, wg, wu, wd):
        rows, dim = x.shape
        dk = dim // 4
        fq = wg.shape[1] // 2
        nch = fq // CW
        ns = dk // CW
        bf16 = jnp.bfloat16
        dma = pltpu.SemaphoreType.DMA
        shapes = [
            (rows, dim),
            (nch, dk, 2 * CW), (nch, dk, 2 * CW), (nch, dk, 2 * CW),
            (3, ns, fq, CW),
            (4 * rows, fq),
            (4, 4 * ns, rows, CW),
            (4 * ns, rows, CW), (4 * ns, rows, CW), (4 * ns, rows, CW),
        ]
        outs = pl.pallas_call(
            kernel,
            out_shape=[jax.ShapeDtypeStruct(s, bf16) for s in shapes],
            in_specs=[pl.BlockSpec(memory_space=pl.ANY)] * 4,
            out_specs=[pl.BlockSpec(memory_space=pl.ANY)] * len(shapes),
            scratch_shapes=[
                pltpu.VMEM((4 * rows, dim), bf16),
                pltpu.VMEM((2, dim, 2 * CW), bf16),
                pltpu.VMEM((2, rows, CW), bf16),
                dma, dma((3,)), dma((6,)), dma((4,)), dma((4,)), dma((4,)),
                dma((nch,)), dma((nch,)), dma((nch,)), dma((ns,)), dma((ns,)), dma((ns,)),
                dma((2,)), dma((2,)), dma((4,)), dma((2,)),
                dma((4 * ns,)), dma((4 * ns,)), dma((4 * ns,)), dma((2,)), dma((4,)), dma((2,)),
            ],
            compiler_params=pltpu.CompilerParams(
                collective_id=0, has_side_effects=True, vmem_limit_bytes=67043328),
            cost_estimate=pl.CostEstimate(
                flops=6 * rows * 4 * dim * fq, bytes_accessed=4 * rows * dim * 2, transcendentals=0),
        )(x, wg, wu, wd)
        return outs[0]

    return jax.shard_map(body, mesh=mesh, in_specs=(P(("dp", "tp"), None), P("dp", "tp"), P("dp", "tp"), P("tp", "dp")), out_specs=P(("dp", "tp"), None), check_vma=False)
```

time: 3690 us -> 1180 us (0.32)
  waiting for transfers between devices: 2700 us -> 0 us
  Pallas kernels: 0 us -> 1170 us
  matrix products: 493 us -> 0 us
  blocking collectives: 361 us -> 0 us
  local copies, waits for them, and re-layouts: 81 us -> 8.78 us
  other arithmetic: 37 us -> 0 us
    reduce_scatter x2 -> x0, waiting for transfers between devices: 1320 us -> none  [the longest x1 742 us: body(): lax.psum_scatter(pb, 'dp', scatter_dimension=0, tiled=True)]
    pallas_call x0 -> x1, Pallas kernels: none -> 1170 us  [body(): pl.pallas_call(kernel, out_shape=[jax.ShapeDtypeStruct(s, bf16) for s in...]
    all_gather x2 -> x0, waiting for transfers between devices: 923 us -> none  [the longest x1 675 us: body(): hg = lax.all_gather(h, 'dp', axis=0, tiled=True)]
    dot_general x3 -> x0, matrix products: 493 us -> none  [the longest x1 164 us: body(): jnp.dot(hg, wd, preferred_element_type=jnp.float32).astype(jnp.bfloat16)]
    unnamed x6 -> x0, waiting for transfers between devices: 461 us -> none
    all_to_all x2 -> x0, blocking collectives: 361 us -> none  [the longest x1 240 us: body(): xc = lax.all_to_all(xt, 'dp', 1, 0, tiled=True)]
    convert_element_type x2 -> x0, other arithmetic: 37 us -> none  [the longest x1 29.9 us: body(): h = (jax.nn.silu(a) * b).astype(jnp.bfloat16)]
  transfers between devices with their start and end apart: 5 -> 0, of which waited for: 5 -> 0; matrix products, arithmetic and copies ran while one was open for 4% -> 0% of each run, Pallas kernels for 0% -> 0%
where the time goes in v2:
time: 1180 us
  Pallas kernels  1170 us (99%)
    pallas_call x1, Pallas kernels, body(): pl.pallas_call(kernel, out_shape=[jax.ShapeDtypeStruct(s, bf16) for s in...  1170 us

profile of v2, /device:TPU:0, one launch (start us, length us, event | category | flops | bytes accessed | tf_op | source)
XLA Modules:
  0.0 1178.2 jit_solution(15047476842721115384)
XLA Ops:
  0.0 1169.4 %shard_map.46 = (bf16[1024,5120]{1,0:T(8,128)(2,1)}, bf16[14,1280,512]{2,1,0:T(8,128)(2,1)}, bf16[14,1280,512]{2,1,0:T(8,128)(2,1)}, bf16[14,1280,512]{2,1,0:T(8...) custom-call(bf16[1024,5120]{1,0:T(8,128)(2,1)} %x.1, ...), custom_call_target="tpu_custom_call" | custom-call | flops 450971566080 | bytes 41943040 | tf_op jit(solution)/shard_map/pallas_call | solution.py:360
  1169.4 8.8 copy.6
